TPU v7x, 32 devices: a whole 2x2x4 slice. The times are simulated.
32 devices in a mesh: row: 8 (over z, x), col: 4 (over y, core).
Axes of the slice: x: 2, y: 2, z: 4, core: 2. Of those that a mesh axis runs over, the one named last changes fastest.
Arguments:
- tensor: float32 [32, 1024, 1024], P(None, 'row', 'col'), may hold values from -6 to 6
- initial_first: float32 [1024, 256], P('row'), may hold values from -6 to 6
- initial_second: float32 [1024, 256], P('col'), may hold values from -6 to 6
Outputs:
- factor_first: float32 [1024, 256], P('row')
- factor_second: float32 [1024, 256], P('col')
- factor_frames: float32 [32, 256], replicated
- weights: float32 [256], replicated
All inputs are finite; a program needn't handle non-finite values.
Results may differ from a plain program's by a relative error of at most 0.00024.
Values sent between devices are 32-bit elements; how exact they have to be, the bound alone decides.
A program may use at most 128 MiB of HBM per device.

v0:
```python
import math
import jax
import jax.numpy as jnp
from jax import lax
from jax.sharding import PartitionSpec as P

PASSES = 2
epsilon = 1e-06


def solve_gram(partials, hadamard):
    factor_lower = jnp.linalg.cholesky(hadamard)
    midway = lax.linalg.triangular_solve(
        factor_lower, partials, left_side=False, lower=True, transpose_a=True
    )
    return lax.linalg.triangular_solve(
        factor_lower, midway, left_side=False, lower=True, transpose_a=False
    )


def local_gram(matrix):
    return jnp.dot(matrix.T, matrix, precision=lax.Precision.HIGHEST)


def normalize_second(unscaled, row_count):
    squares = lax.psum(jnp.sum(unscaled * unscaled, axis=0), "col")
    scaling = jnp.sqrt(squares / row_count + epsilon)
    normed = unscaled / scaling
    gram_new = lax.psum(local_gram(normed), "col") / row_count
    return (normed, gram_new)


def body(tensor, initial_first, initial_second):
    highest = lax.Precision.HIGHEST
    frames = tensor.shape[0]
    rows_first = tensor.shape[1] * lax.axis_size("row")
    rows_second = tensor.shape[2] * lax.axis_size("col")
    first_gram = lax.psum(local_gram(initial_first), "row") / rows_first
    second = initial_second
    second_gram = lax.psum(local_gram(initial_second), "col") / rows_second
    contracted = jnp.einsum("kij,ir->kjr", tensor, initial_first, precision=highest)
    for repeat in range(PASSES):
        frame_terms = jnp.einsum("kjr,jr->kr", contracted, second, precision=highest)
        frame_sums = lax.psum(frame_terms, ("row", "col"))
        frame_raw = solve_gram(frame_sums, first_gram * second_gram) / math.sqrt(
            rows_first * rows_second
        )
        frame_scaling = jnp.sqrt(jnp.mean(frame_raw * frame_raw, axis=0) + epsilon)
        factor_frames = frame_raw / frame_scaling
        frame_gram = local_gram(factor_frames) / frames
        second_terms = jnp.einsum("kjr,kr->jr", contracted, factor_frames, precision=highest)
        hadamard = first_gram * frame_gram
        own_rows = lax.psum_scatter(second_terms, "row", scatter_dimension=0, tiled=True)
        solved_rows = solve_gram(own_rows, hadamard) / math.sqrt(rows_first * frames)
        second_raw = lax.all_gather(solved_rows, "row", axis=0, tiled=True)
        second, second_gram = normalize_second(second_raw, rows_second)
    second_contracted = jnp.einsum("kij,jr->kir", tensor, second, precision=highest)
    first_terms = jnp.einsum("kir,kr->ir", second_contracted, factor_frames, precision=highest)
    hadamard = second_gram * frame_gram
    own_rows = lax.psum_scatter(first_terms, "col", scatter_dimension=0, tiled=True)
    solved_rows = solve_gram(own_rows, hadamard) / math.sqrt(rows_second * frames)
    first_raw = lax.all_gather(solved_rows, "col", axis=0, tiled=True)
    squares = lax.psum(jnp.sum(first_raw * first_raw, axis=0), "row")
    weights = jnp.sqrt(squares / rows_first + epsilon)
    factor_first = first_raw / weights
    return (factor_first, second, factor_frames, weights)


def solution(mesh):
    placed = (P(None, "row", "col"), P("row", None), P("col", None))
    return jax.shard_map(
        body,
        mesh=mesh,
        in_specs=placed,
        out_specs=(P("row", None), P("col", None), P(), P()),
        check_vma=False,
    )
```

profile of v0, /device:TPU:0, one launch (start us, length us, event | category | flops | bytes accessed | tf_op | source)
XLA Modules:
  0.0 647.6 jit_solution(8311122888523446965)
XLA Ops:
  7.2 2.4 fusion.93
  10.9 10.7 %multiply_reduce_fusion.3 = (f32[256,32]{0,1:T(8,128)S(1)}, f32[32,256,256]{2,1,0:T(8,128)}) fusion(f32[256,256]{0,1:T(8,128)} %bitcast.270, f32[32,128,256]{2,1,0:T(8,128)} %param.8, f32[128,256]{1,0:T(8,128)S(1)} %copy-done), kind=kOutput, calls=%fused_computation.13 | convolution fusion | flops 3225411584 | bytes 13008896 | tf_op jit(solution)/shard_map/kij,ir->kjr/dot_general | solution.py:41
  21.7 43.2 %psum.65 = f32[32,256]{0,1:T(8,128)S(1)} all-reduce(f32[32,256]{0,1:T(8,128)S(1)} %bitcast.276), channel_id=1, replica_groups=mesh['row'=8,'col'=4] {'row','col'}, use_global_device_ids=true, to_apply=%region_6.0 | all-reduce | flops 8192 | bytes 65536 | tf_op jit(solution)/shard_map/psum | solution.py:44
  65.0 55.4 %all-reduce.6.cloned.1.call-done = f32[256,256]{0,1:T(8,128)} async-done(((f32[256,256]{0,1:T(8,128)}), f32[256,256]{0,1:T(8,128)}) %all-reduce.6.cloned.1.call-update) | async-done | bytes 262160 | tf_op jit(solution)/shard_map/psum | solution.py:38
  121.7 11.7 %cholesky.256 = f32[128,128]{1,0:T(8,128)S(1)} custom-call(f32[128,128]{1,0:T(8,128)S(1)} %cholesky.422), custom_call_target="Cholesky" | custom-call | tf_op jit(solution)/shard_map/jit(cholesky)/cholesky | solution.py:12
  133.5 9.8 %custom-call.26 = f32[1,128,128]{1,2,0:T(8,128)S(1)} custom-call(f32[1,128,128]{2,1,0:T(8,128)S(1)} %get-tuple-element.150), custom_call_target="InvertDiagBlocksLowerTriangular" | custom-call | tf_op jit(solution)/shard_map/jit(cholesky)/cholesky | solution.py:12
  143.8 11.7 %cholesky.273 = f32[128,128]{1,0:T(8,128)S(1)} custom-call(f32[128,128]{1,0:T(8,128)S(1)} %convolution_subtract_fusion.9), custom_call_target="Cholesky" | custom-call | tf_op jit(solution)/shard_map/jit(cholesky)/cholesky | solution.py:12
  157.6 4.0 while.20
  158.2 1.4 bitcast_dynamic-update-slice_fusion.10
  160.2 1.4 bitcast_dynamic-update-slice_fusion.10
  161.6 20.1 %custom-call.27 = f32[2,128,128]{1,2,0:T(8,128)S(1)} custom-call(f32[2,128,128]{2,1,0:T(8,128)S(1)} %get-tuple-element.71), custom_call_target="InvertDiagBlocksLowerTriangular" | custom-call | tf_op jit(solution)/shard_map/triangular_solve/custom-call.0 | solution.py:13
  183.1 4.9 multiply_reduce_fusion.2
  188.7 11.7 %cholesky.290 = f32[128,128]{1,0:T(8,128)S(1)} custom-call(f32[128,128]{1,0:T(8,128)S(1)} %cholesky.425), custom_call_target="Cholesky" | custom-call | tf_op jit(solution)/shard_map/jit(cholesky)/cholesky | solution.py:12
  200.5 9.8 %custom-call.29 = f32[1,128,128]{1,2,0:T(8,128)S(1)} custom-call(f32[1,128,128]{2,1,0:T(8,128)S(1)} %get-tuple-element.146), custom_call_target="InvertDiagBlocksLowerTriangular" | custom-call | tf_op jit(solution)/shard_map/jit(cholesky)/cholesky | solution.py:12
  210.8 11.7 %cholesky.307 = f32[128,128]{1,0:T(8,128)S(1)} custom-call(f32[128,128]{1,0:T(8,128)S(1)} %convolution_subtract_fusion.7), custom_call_target="Cholesky" | custom-call | tf_op jit(solution)/shard_map/jit(cholesky)/cholesky | solution.py:12
  225.1 4.2 while.21
  225.9 1.4 bitcast_dynamic-update-slice_fusion.11
  227.9 1.4 bitcast_dynamic-update-slice_fusion.11
  229.3 19.7 %custom-call.30 = f32[2,128,128]{1,2,0:T(8,128)S(1)} custom-call(f32[2,128,128]{2,1,0:T(8,128)S(1)} %get-tuple-element.73), custom_call_target="InvertDiagBlocksLowerTriangular" | custom-call | tf_op jit(solution)/shard_map/triangular_solve/custom-call.0 | solution.py:13
  252.6 30.9 %all_gather.9 = f32[256,256]{1,0:T(8,128)S(1)} all-gather(f32[32,256]{1,0:T(8,128)S(1)} %maximum_multiply_fusion.1), channel_id=1, replica_groups=mesh['row'=8,'col'=4] {'row'}, dimensions={0}, use_global_device_ids=true | all-gather | bytes 294912 | tf_op jit(solution)/shard_map/all_gather | solution.py:55
  283.5 5.7 psum.66
  290.6 4.2 multiply_reduce_fusion.1
  294.9 39.1 %psum.68 = f32[32,256]{0,1:T(8,128)S(1)} all-reduce(f32[32,256]{0,1:T(8,128)S(1)} %bitcast.277), channel_id=1, replica_groups=mesh['row'=8,'col'=4] {'row','col'}, use_global_device_ids=true, to_apply=%region_12.16 | all-reduce | flops 8192 | bytes 65536 | tf_op jit(solution)/shard_map/psum | solution.py:44
  335.3 11.7 %cholesky.324 = f32[128,128]{1,0:T(8,128)S(1)} custom-call(f32[128,128]{1,0:T(8,128)S(1)} %cholesky.428), custom_call_target="Cholesky" | custom-call | tf_op jit(solution)/shard_map/jit(cholesky)/cholesky | solution.py:12
  347.0 9.8 %custom-call.32 = f32[1,128,128]{1,2,0:T(8,128)S(1)} custom-call(f32[1,128,128]{2,1,0:T(8,128)S(1)} %get-tuple-element.142), custom_call_target="InvertDiagBlocksLowerTriangular" | custom-call | tf_op jit(solution)/shard_map/jit(cholesky)/cholesky | solution.py:12
  357.3 11.7 %cholesky.341 = f32[128,128]{1,0:T(8,128)S(1)} custom-call(f32[128,128]{1,0:T(8,128)S(1)} %convolution_subtract_fusion.5), custom_call_target="Cholesky" | custom-call | tf_op jit(solution)/shard_map/jit(cholesky)/cholesky | solution.py:12
  371.7 4.0 while.22
  372.3 1.4 bitcast_dynamic-update-slice_fusion.12
  375.7 20.1 %custom-call.33 = f32[2,128,128]{1,2,0:T(8,128)S(1)} custom-call(f32[2,128,128]{2,1,0:T(8,128)S(1)} %get-tuple-element.75), custom_call_target="InvertDiagBlocksLowerTriangular" | custom-call | tf_op jit(solution)/shard_map/triangular_solve/custom-call.0 | solution.py:13
  397.3 4.9 multiply_reduce_fusion
  402.9 11.7 %cholesky.358 = f32[128,128]{1,0:T(8,128)S(1)} custom-call(f32[128,128]{1,0:T(8,128)S(1)} %cholesky.431), custom_call_target="Cholesky" | custom-call | tf_op jit(solution)/shard_map/jit(cholesky)/cholesky | solution.py:12
  414.7 9.8 %custom-call.35 = f32[1,128,128]{1,2,0:T(8,128)S(1)} custom-call(f32[1,128,128]{2,1,0:T(8,128)S(1)} %get-tuple-element.138), custom_call_target="InvertDiagBlocksLowerTriangular" | custom-call | tf_op jit(solution)/shard_map/jit(cholesky)/cholesky | solution.py:12
  424.9 11.7 %cholesky.375 = f32[128,128]{1,0:T(8,128)S(1)} custom-call(f32[128,128]{1,0:T(8,128)S(1)} %convolution_subtract_fusion.3), custom_call_target="Cholesky" | custom-call | tf_op jit(solution)/shard_map/jit(cholesky)/cholesky | solution.py:12
  439.3 4.2 while.23
  443.5 19.7 %custom-call.36 = f32[2,128,128]{1,2,0:T(8,128)S(1)} custom-call(f32[2,128,128]{2,1,0:T(8,128)S(1)} %get-tuple-element.77), custom_call_target="InvertDiagBlocksLowerTriangular" | custom-call | tf_op jit(solution)/shard_map/triangular_solve/custom-call.0 | solution.py:13
  463.2 2.9 reduce-scatter.12.cloned.1.call-done
  468.9 30.9 %all_gather.10 = f32[256,256]{1,0:T(8,128)S(1)} all-gather(f32[32,256]{1,0:T(8,128)S(1)} %maximum_multiply_fusion.3), channel_id=1, replica_groups=mesh['row'=8,'col'=4] {'row'}, dimensions={0}, use_global_device_ids=true | all-gather | bytes 294912 | tf_op jit(solution)/shard_map/all_gather | solution.py:55
  499.8 5.7 psum.69
  505.5 10.0 %fusion.4 = f32[256,32,128]{2,0,1:T(8,128)} fusion(f32[32,128,256]{2,1,0:T(8,128)} %param.8, f32[256,256]{1,0:T(8,128)S(1)} %broadcast_divide_fusion), kind=kOutput, calls=%fused_computation.40 | convolution fusion | flops 3221225472 | bytes 8650752 | tf_op jit(solution)/shard_map/kij,jr->kir/dot_general | solution.py:57
  516.8 8.2 %fusion = f32[256,1,128]{2,1,0:T(1,128)S(1)} fusion(f32[32,256,1]{0,2,1:T(1,128)S(1)} %copy.67, f32[256,32,128]{2,0,1:T(8,128)} %fusion.4), kind=kOutput, calls=%fused_computation.14 | convolution fusion | flops 12582912 | bytes 4358144 | tf_op jit(solution)/shard_map/kir,kr->ir/dot_general | solution.py:58
  525.8 22.6 %all-reduce.12.cloned.1.call-done = f32[256,256]{0,1:T(8,128)} async-done(((f32[256,256]{0,1:T(8,128)}), f32[256,256]{0,1:T(8,128)}) %all-reduce.12.cloned.1.call-update) | async-done | bytes 262160 | tf_op jit(solution)/shard_map/psum | solution.py:29
  549.7 11.7 %cholesky.392 = f32[128,128]{1,0:T(8,128)S(1)} custom-call(f32[128,128]{1,0:T(8,128)S(1)} %cholesky.434), custom_call_target="Cholesky" | custom-call | tf_op jit(solution)/shard_map/jit(cholesky)/cholesky | solution.py:12
  561.4 9.8 %custom-call.38 = f32[1,128,128]{1,2,0:T(8,128)S(1)} custom-call(f32[1,128,128]{2,1,0:T(8,128)S(1)} %get-tuple-element.134), custom_call_target="InvertDiagBlocksLowerTriangular" | custom-call | tf_op jit(solution)/shard_map/jit(cholesky)/cholesky | solution.py:12
  571.7 11.7 %cholesky.409 = f32[128,128]{1,0:T(8,128)S(1)} custom-call(f32[128,128]{1,0:T(8,128)S(1)} %convolution_subtract_fusion.1), custom_call_target="Cholesky" | custom-call | tf_op jit(solution)/shard_map/jit(cholesky)/cholesky | solution.py:12
  586.2 4.0 while.24
  590.2 19.9 %custom-call.39 = f32[2,128,128]{1,2,0:T(8,128)S(1)} custom-call(f32[2,128,128]{2,1,0:T(8,128)S(1)} %get-tuple-element.79), custom_call_target="InvertDiagBlocksLowerTriangular" | custom-call | tf_op jit(solution)/shard_map/triangular_solve/custom-call.0 | solution.py:13
  613.0 5.4 all_gather.11
  618.4 21.4 %psum.71 = f32[256]{0:T(256)S(1)} all-reduce(f32[256]{0:T(256)S(1)} %multiply_reduce_fusion.6), channel_id=1, replica_groups=mesh['row'=8,'col'=4] {'row'}, use_global_device_ids=true, to_apply=%region_20.24 | all-reduce | flops 256 | bytes 2048 | tf_op jit(solution)/shard_map/psum | solution.py:63
  (180 shorter events, 44.5 us)
Async XLA Ops:
  7.2 2.5 copy-start
  7.2 57.8 %all-reduce.8.cloned.1.call-start = ((), (), s32[]{:S(2)}) async-start(), calls=%async_computation.4 | async-start | bytes 524288 | tf_op jit(solution)/shard_map/psum | solution.py:40
  9.6 110.8 %all-reduce.6.cloned.1.call-start = ((), (), s32[]{:S(2)}) async-start(), calls=%async_computation.3 | async-start | bytes 524288 | tf_op jit(solution)/shard_map/psum | solution.py:38
  10.8 239.0 %reduce-scatter.10.cloned.1.call-start = ((), (), s32[]{:S(2)}) async-start(), calls=%async_computation.7 | async-start | bytes 294912
  120.4 67.6 %copy-start.1 = (f32[256,256]{0,1:T(8,128)S(1)}, f32[256,256]{0,1:T(8,128)}, u32[]{:S(2)}) copy-start(f32[256,256]{0,1:T(8,128)} %all-reduce.6.cloned.1.call-done) | copy-start | bytes 786436
  188.0 146.1 %all-reduce.10.cloned.1.call-start = ((), (), s32[]{:S(2)}) async-start(), calls=%async_computation.5 | async-start | bytes 524288 | tf_op jit(solution)/shard_map/psum | solution.py:29
  290.6 175.4 %reduce-scatter.12.cloned.1.call-start = ((), (), s32[]{:S(2)}) async-start(), calls=%async_computation.8 | async-start | bytes 294912
  397.2 118.2 %copy-start.3 = (f32[32,256]{1,0:T(8,128)}, f32[32,256]{1,0:T(8,128)S(1)}, u32[]{:S(2)}) copy-start(f32[32,256]{1,0:T(8,128)S(1)} %fusion.78) | copy-start | bytes 98308
  402.2 146.3 %all-reduce.12.cloned.1.call-start = ((), (), s32[]{:S(2)}) async-start(), calls=%async_computation.6 | async-start | bytes 524288 | tf_op jit(solution)/shard_map/psum | solution.py:29
  505.5 44.2 %copy-start.2 = (f32[256,256]{1,0:T(8,128)}, f32[256,256]{1,0:T(8,128)S(1)}, u32[]{:S(2)}) copy-start(f32[256,256]{1,0:T(8,128)S(1)} %broadcast_divide_fusion) | copy-start | bytes 786436
  516.8 93.4 %reduce-scatter.14.cloned.1.call-start = ((), (), s32[]{:S(2)}) async-start(), calls=%async_computation.9 | async-start | bytes 163840
  639.8 0.7 copy-start.4
Sparse Core Ops, SparseCore 0:
  10.9 34.9 all-reduce.7
  49.3 71.0 all-reduce.5
  188.1 61.6 reduce-scatter.9
  290.7 31.6 all-reduce.9
  402.3 63.6 reduce-scatter.11
  516.9 31.5 all-reduce.11
  551.5 19.8 reduce-scatter.13
where the time goes:
time: 653 us; the launch traced here: 648 us
  other arithmetic  290 us (44%)
  blocking collectives  182 us (28%)
  waiting for transfers between devices  81.9 us (13%)
  matrix products  46.5 us (7%)
  local copies, waits for them, and re-layouts  24.2 us (4%)
  between operations  21.7 us (3%)
    another operation x34, other arithmetic, solve_gram(): factor_lower = jnp.linalg.cholesky(hadamard)  172 us
    another operation x11, other arithmetic, solve_gram(): lax.linalg.triangular_solve(factor_lower, partials, left_side=False, lowe...  99.6 us
    psum x2, blocking collectives, body(): frame_sums = lax.psum(frame_terms, ('row', 'col'))  82.3 us
    all_gather x2, blocking collectives, body(): second_raw = lax.all_gather(solved_rows, 'row', axis=0, tiled=True)  61.7 us
    psum x1, waiting for transfers between devices, body(): first_gram = lax.psum(local_gram(initial_first), 'row') / rows_first  55.4 us
    psum x2, waiting for transfers between devices, normalize_second(): gram_new = lax.psum(local_gram(normed), 'col') / row_count  22.7 us
    another operation x39, local copies, waits for them, and re-layouts, solve_gram(): lax.linalg.triangular_solve(factor_lower, partials, left_side=False, lowe...  22 us
    psum x1, blocking collectives, body(): squares = lax.psum(jnp.sum(first_raw * first_raw, axis=0), 'row')  21.4 us
  transfers between devices with their start and end apart: 7, of which 4 were waited for; matrix products, arithmetic and copies ran while one was open for 32% of the time, Pallas kernels for 0%

commit v1 on v0

--- a/solution.py
+++ b/solution.py
@@ -52,7 +52,14 @@
         hadamard = first_gram * frame_gram
         own_rows = lax.psum_scatter(second_terms, "row", scatter_dimension=0, tiled=True)
         solved_rows = solve_gram(own_rows, hadamard) / math.sqrt(rows_first * frames)
-        second_raw = lax.all_gather(solved_rows, "row", axis=0, tiled=True)
+        ring = [solved_rows]
+        for hop in range(7):
+            ring.append(lax.ppermute(ring[-1], "row", [(dev, (dev + 1) % 8) for dev in range(8)]))
+        second_raw = jnp.roll(
+            jnp.concatenate(ring[::-1], axis=0),
+            (lax.axis_index("row") + 1) * ring[0].shape[0],
+            axis=0,
+        )
         second, second_gram = normalize_second(second_raw, rows_second)
     second_contracted = jnp.einsum("kij,jr->kir", tensor, second, precision=highest)
     first_terms = jnp.einsum("kir,kr->ir", second_contracted, factor_frames, precision=highest)

time: 653 us -> 683 us (1.046)
  waiting for transfers between devices: 81.9 us -> 171 us
  blocking collectives: 182 us -> 119 us
    ppermute x0 -> x14, waiting for transfers between devices: none -> 90.1 us  [body(): lax.ppermute(ring[-1], 'row', [(dev, (dev + 1) % 8) for dev in range(8)])]
    all_gather x2 -> x0, blocking collectives: 61.7 us -> none  [body(): second_raw = lax.all_gather(solved_rows, 'row', axis=0, tiled=True)]
  transfers between devices with their start and end apart: 7 -> 21, of which waited for: 4 -> 18; matrix products, arithmetic and copies ran while one was open for 32% -> 30% of each run, Pallas kernels for 0% -> 0%
where the time goes in v1:
time: 683 us; the launch traced here: 678 us
  other arithmetic  290 us (42%)
  waiting for transfers between devices  171 us (25%)
  blocking collectives  119 us (17%)
  matrix products  46.5 us (7%)
  local copies, waits for them, and re-layouts  24.2 us (4%)
  between operations  21.8 us (3%)
    another operation x34, other arithmetic, solve_gram(): factor_lower = jnp.linalg.cholesky(hadamard)  172 us
    another operation x11, other arithmetic, solve_gram(): lax.linalg.triangular_solve(factor_lower, partials, left_side=False, lowe...  99.6 us
    ppermute x14, waiting for transfers between devices, body(): lax.ppermute(ring[-1], 'row', [(dev, (dev + 1) % 8) for dev in range(8)])  90.1 us
    psum x2, blocking collectives, body(): frame_sums = lax.psum(frame_terms, ('row', 'col'))  81.2 us
    psum x1, waiting for transfers between devices, body(): first_gram = lax.psum(local_gram(initial_first), 'row') / rows_first  55.4 us
    another operation x39, local copies, waits for them, and re-layouts, solve_gram(): lax.linalg.triangular_solve(factor_lower, partials, left_side=False, lowe...  22 us
    psum x1, blocking collectives, body(): squares = lax.psum(jnp.sum(first_raw * first_raw, axis=0), 'row')  21.4 us
    psum x2, waiting for transfers between devices, normalize_second(): gram_new = lax.psum(local_gram(normed), 'col') / row_count  21 us
  transfers between devices with their start and end apart: 21, of which 18 were waited for; matrix products, arithmetic and copies ran while one was open for 30% of the time, Pallas kernels for 0%

profile of v1, /device:TPU:0, one launch (start us, length us, event | category | flops | bytes accessed | tf_op | source)
XLA Modules:
  0.0 677.5 jit_solution(12458868012284297999)
XLA Ops:
  10.9 10.7 %multiply_reduce_fusion.3 = (f32[256,32]{0,1:T(8,128)S(1)}, f32[32,256,256]{2,1,0:T(8,128)}) fusion(f32[256,256]{0,1:T(8,128)} %bitcast.270, f32[32,128,256]{2,1,0:T(8,128)} %param.10, f32[128,256]{1,0:T(8,128)S(1)} %copy-done), kind=kOutput, calls=%fused_computation.13 | convolution fusion | flops 3225411584 | bytes 13008896 | tf_op jit(solution)/shard_map/kij,ir->kjr/dot_general | solution.py:41
  21.7 43.2 %psum.65 = f32[32,256]{0,1:T(8,128)S(1)} all-reduce(f32[32,256]{0,1:T(8,128)S(1)} %bitcast.276), channel_id=1, replica_groups=mesh['row'=8,'col'=4] {'row','col'}, use_global_device_ids=true, to_apply=%region_6.8 | all-reduce | flops 8192 | bytes 65536 | tf_op jit(solution)/shard_map/psum | solution.py:44
  65.0 55.4 %all-reduce.6.cloned.1.call-done = f32[256,256]{0,1:T(8,128)} async-done(((f32[256,256]{0,1:T(8,128)}), f32[256,256]{0,1:T(8,128)}) %all-reduce.6.cloned.1.call-update) | async-done | bytes 262160 | tf_op jit(solution)/shard_map/psum | solution.py:38
  121.7 11.7 %cholesky.256 = f32[128,128]{1,0:T(8,128)S(1)} custom-call(f32[128,128]{1,0:T(8,128)S(1)} %cholesky.422), custom_call_target="Cholesky" | custom-call | tf_op jit(solution)/shard_map/jit(cholesky)/cholesky | solution.py:12
  133.5 9.8 %custom-call.26 = f32[1,128,128]{1,2,0:T(8,128)S(1)} custom-call(f32[1,128,128]{2,1,0:T(8,128)S(1)} %get-tuple-element.153), custom_call_target="InvertDiagBlocksLowerTriangular" | custom-call | tf_op jit(solution)/shard_map/jit(cholesky)/cholesky | solution.py:12
  143.8 11.7 %cholesky.273 = f32[128,128]{1,0:T(8,128)S(1)} custom-call(f32[128,128]{1,0:T(8,128)S(1)} %convolution_subtract_fusion.9), custom_call_target="Cholesky" | custom-call | tf_op jit(solution)/shard_map/jit(cholesky)/cholesky | solution.py:12
  161.6 20.1 %custom-call.27 = f32[2,128,128]{1,2,0:T(8,128)S(1)} custom-call(f32[2,128,128]{2,1,0:T(8,128)S(1)} %get-tuple-element.72), custom_call_target="InvertDiagBlocksLowerTriangular" | custom-call | tf_op jit(solution)/shard_map/triangular_solve/custom-call.0 | solution.py:13
  183.1 4.9 multiply_reduce_fusion.2
  188.7 11.7 %cholesky.290 = f32[128,128]{1,0:T(8,128)S(1)} custom-call(f32[128,128]{1,0:T(8,128)S(1)} %cholesky.425), custom_call_target="Cholesky" | custom-call | tf_op jit(solution)/shard_map/jit(cholesky)/cholesky | solution.py:12
  200.5 9.8 %custom-call.29 = f32[1,128,128]{1,2,0:T(8,128)S(1)} custom-call(f32[1,128,128]{2,1,0:T(8,128)S(1)} %get-tuple-element.149), custom_call_target="InvertDiagBlocksLowerTriangular" | custom-call | tf_op jit(solution)/shard_map/jit(cholesky)/cholesky | solution.py:12
  210.8 11.7 %cholesky.307 = f32[128,128]{1,0:T(8,128)S(1)} custom-call(f32[128,128]{1,0:T(8,128)S(1)} %convolution_subtract_fusion.7), custom_call_target="Cholesky" | custom-call | tf_op jit(solution)/shard_map/jit(cholesky)/cholesky | solution.py:12
  229.3 19.7 %custom-call.30 = f32[2,128,128]{1,2,0:T(8,128)S(1)} custom-call(f32[2,128,128]{2,1,0:T(8,128)S(1)} %get-tuple-element.74), custom_call_target="InvertDiagBlocksLowerTriangular" | custom-call | tf_op jit(solution)/shard_map/triangular_solve/custom-call.0 | solution.py:13
  254.1 5.2 collective-permute-done
  259.3 6.6 collective-permute-done.1
  265.9 6.8 %collective-permute-done.2 = f32[32,256]{1,0:T(8,128)S(1)} collective-permute-done((f32[32,256]{1,0:T(8,128)S(1)}, f32[32,256]{1,0:T(8,128)S(1)}, u32[]{:S(2)}, u32[]{:S(2)}) %collective-permute-start.2) | collective-permute-done | bytes 32800 | tf_op jit(solution)/shard_map/ppermute | solution.py:57
  272.8 6.6 collective-permute-done.3
  279.4 6.6 collective-permute-done.4
  286.0 6.6 collective-permute-done.5
  292.6 6.6 collective-permute-done.6
  299.4 5.7 psum.66
  306.5 4.2 multiply_reduce_fusion.1
  310.9 38.0 %psum.68 = f32[32,256]{0,1:T(8,128)S(1)} all-reduce(f32[32,256]{0,1:T(8,128)S(1)} %bitcast.277), channel_id=1, replica_groups=mesh['row'=8,'col'=4] {'row','col'}, use_global_device_ids=true, to_apply=%region_12.0 | all-reduce | flops 8192 | bytes 65536 | tf_op jit(solution)/shard_map/psum | solution.py:44
  350.1 11.7 %cholesky.324 = f32[128,128]{1,0:T(8,128)S(1)} custom-call(f32[128,128]{1,0:T(8,128)S(1)} %cholesky.428), custom_call_target="Cholesky" | custom-call | tf_op jit(solution)/shard_map/jit(cholesky)/cholesky | solution.py:12
  361.9 9.8 %custom-call.32 = f32[1,128,128]{1,2,0:T(8,128)S(1)} custom-call(f32[1,128,128]{2,1,0:T(8,128)S(1)} %get-tuple-element.145), custom_call_target="InvertDiagBlocksLowerTriangular" | custom-call | tf_op jit(solution)/shard_map/jit(cholesky)/cholesky | solution.py:12
  372.1 11.7 %cholesky.341 = f32[128,128]{1,0:T(8,128)S(1)} custom-call(f32[128,128]{1,0:T(8,128)S(1)} %convolution_subtract_fusion.5), custom_call_target="Cholesky" | custom-call | tf_op jit(solution)/shard_map/jit(cholesky)/cholesky | solution.py:12
  390.5 20.1 %custom-call.33 = f32[2,128,128]{1,2,0:T(8,128)S(1)} custom-call(f32[2,128,128]{2,1,0:T(8,128)S(1)} %get-tuple-element.76), custom_call_target="InvertDiagBlocksLowerTriangular" | custom-call | tf_op jit(solution)/shard_map/triangular_solve/custom-call.0 | solution.py:13
  412.1 4.9 multiply_reduce_fusion
  417.6 11.7 %cholesky.358 = f32[128,128]{1,0:T(8,128)S(1)} custom-call(f32[128,128]{1,0:T(8,128)S(1)} %cholesky.431), custom_call_target="Cholesky" | custom-call | tf_op jit(solution)/shard_map/jit(cholesky)/cholesky | solution.py:12
  429.4 9.8 %custom-call.35 = f32[1,128,128]{1,2,0:T(8,128)S(1)} custom-call(f32[1,128,128]{2,1,0:T(8,128)S(1)} %get-tuple-element.141), custom_call_target="InvertDiagBlocksLowerTriangular" | custom-call | tf_op jit(solution)/shard_map/jit(cholesky)/cholesky | solution.py:12
  439.7 11.7 %cholesky.375 = f32[128,128]{1,0:T(8,128)S(1)} custom-call(f32[128,128]{1,0:T(8,128)S(1)} %convolution_subtract_fusion.3), custom_call_target="Cholesky" | custom-call | tf_op jit(solution)/shard_map/jit(cholesky)/cholesky | solution.py:12
  458.2 19.7 %custom-call.36 = f32[2,128,128]{1,2,0:T(8,128)S(1)} custom-call(f32[2,128,128]{2,1,0:T(8,128)S(1)} %get-tuple-element.78), custom_call_target="InvertDiagBlocksLowerTriangular" | custom-call | tf_op jit(solution)/shard_map/triangular_solve/custom-call.0 | solution.py:13
  486.1 5.2 collective-permute-done.7
  491.3 6.6 collective-permute-done.8
  497.9 6.8 %collective-permute-done.9 = f32[32,256]{1,0:T(8,128)S(1)} collective-permute-done((f32[32,256]{1,0:T(8,128)S(1)}, f32[32,256]{1,0:T(8,128)S(1)}, u32[]{:S(2)}, u32[]{:S(2)}) %collective-permute-start.9) | collective-permute-done | bytes 32800 | tf_op jit(solution)/shard_map/ppermute | solution.py:57
  504.8 6.6 collective-permute-done.10
  511.4 6.6 collective-permute-done.11
  518.0 6.6 collective-permute-done.12
  524.7 6.5 collective-permute-done.13
  531.4 5.7 psum.69
  537.2 10.0 %fusion.6 = f32[256,32,128]{2,0,1:T(8,128)} fusion(f32[32,128,256]{2,1,0:T(8,128)} %param.10, f32[256,256]{1,0:T(8,128)S(1)} %broadcast_divide_fusion), kind=kOutput, calls=%fused_computation.46 | convolution fusion | flops 3221225472 | bytes 8650752 | tf_op jit(solution)/shard_map/kij,jr->kir/dot_general | solution.py:64
  548.5 8.2 %fusion = f32[256,1,128]{2,1,0:T(1,128)S(1)} fusion(f32[32,256,1]{0,2,1:T(1,128)S(1)} %copy.67, f32[256,32,128]{2,0,1:T(8,128)} %fusion.6), kind=kOutput, calls=%fused_computation.14 | convolution fusion | flops 12582912 | bytes 4358144 | tf_op jit(solution)/shard_map/kir,kr->ir/dot_general | solution.py:65
  557.5 20.9 %all-reduce.12.cloned.1.call-done = f32[256,256]{0,1:T(8,128)} async-done(((f32[256,256]{0,1:T(8,128)}), f32[256,256]{0,1:T(8,128)}) %all-reduce.12.cloned.1.call-update) | async-done | bytes 262160 | tf_op jit(solution)/shard_map/psum | solution.py:29
  579.6 11.7 %cholesky.392 = f32[128,128]{1,0:T(8,128)S(1)} custom-call(f32[128,128]{1,0:T(8,128)S(1)} %cholesky.434), custom_call_target="Cholesky" | custom-call | tf_op jit(solution)/shard_map/jit(cholesky)/cholesky | solution.py:12
  591.4 9.8 %custom-call.38 = f32[1,128,128]{1,2,0:T(8,128)S(1)} custom-call(f32[1,128,128]{2,1,0:T(8,128)S(1)} %get-tuple-element.137), custom_call_target="InvertDiagBlocksLowerTriangular" | custom-call | tf_op jit(solution)/shard_map/jit(cholesky)/cholesky | solution.py:12
  601.7 11.7 %cholesky.409 = f32[128,128]{1,0:T(8,128)S(1)} custom-call(f32[128,128]{1,0:T(8,128)S(1)} %convolution_subtract_fusion.1), custom_call_target="Cholesky" | custom-call | tf_op jit(solution)/shard_map/jit(cholesky)/cholesky | solution.py:12
  620.1 19.9 %custom-call.39 = f32[2,128,128]{1,2,0:T(8,128)S(1)} custom-call(f32[2,128,128]{2,1,0:T(8,128)S(1)} %get-tuple-element.80), custom_call_target="InvertDiagBlocksLowerTriangular" | custom-call | tf_op jit(solution)/shard_map/triangular_solve/custom-call.0 | solution.py:13
  642.9 5.4 all_gather.3
  648.4 21.4 %psum.71 = f32[256]{0:T(256)S(1)} all-reduce(f32[256]{0:T(256)S(1)} %multiply_reduce_fusion.6), channel_id=1, replica_groups=mesh['row'=8,'col'=4] {'row'}, use_global_device_ids=true, to_apply=%region_20.25 | all-reduce | flops 256 | bytes 2048 | tf_op jit(solution)/shard_map/psum | solution.py:70
  (222 shorter events, 81.2 us)
Async XLA Ops:
  7.2 2.5 copy-start
  7.2 57.8 %all-reduce.8.cloned.1.call-start = ((), (), s32[]{:S(2)}) async-start(), calls=%async_computation.4 | async-start | bytes 524288 | tf_op jit(solution)/shard_map/psum | solution.py:40
  9.6 110.8 %all-reduce.6.cloned.1.call-start = ((), (), s32[]{:S(2)}) async-start(), calls=%async_computation.3 | async-start | bytes 524288 | tf_op jit(solution)/shard_map/psum | solution.py:38
  10.8 239.0 %reduce-scatter.10.cloned.1.call-start = ((), (), s32[]{:S(2)}) async-start(), calls=%async_computation.7 | async-start | bytes 294912
  120.4 67.6 %copy-start.1 = (f32[256,256]{0,1:T(8,128)S(1)}, f32[256,256]{0,1:T(8,128)}, u32[]{:S(2)}) copy-start(f32[256,256]{0,1:T(8,128)} %all-reduce.6.cloned.1.call-done) | copy-start | bytes 786436
  188.0 160.9 %all-reduce.10.cloned.1.call-start = ((), (), s32[]{:S(2)}) async-start(), calls=%async_computation.5 | async-start | bytes 524288 | tf_op jit(solution)/shard_map/psum | solution.py:29
  252.6 6.7 collective-permute-start
  259.3 6.6 collective-permute-start.1
  265.9 6.9 %collective-permute-start.2 = (f32[32,256]{1,0:T(8,128)S(1)}, f32[32,256]{1,0:T(8,128)S(1)}, u32[]{:S(2)}, u32[]{:S(2)}) collective-permute-start(f32[32,256]{1,0:T(8,128)S(1)} %collective-permute-done.1), channel_id=1, source_target_pairs={{0,4},{4,8},{8,12},{12,16},{16,20},{20,24},{24,28},{28,0},{1,5},{5... | collective-permute-start | bytes 98312 | tf_op jit(solution)/shard_map/ppermute | solution.py:57
  272.8 6.6 collective-permute-start.3
  279.4 6.6 collective-permute-start.4
  286.0 6.6 collective-permute-start.5
  292.6 6.6 collective-permute-start.6
  306.5 175.4 %reduce-scatter.12.cloned.1.call-start = ((), (), s32[]{:S(2)}) async-start(), calls=%async_computation.8 | async-start | bytes 294912
  412.0 135.1 %copy-start.3 = (f32[32,256]{1,0:T(8,128)}, f32[32,256]{1,0:T(8,128)S(1)}, u32[]{:S(2)}) copy-start(f32[32,256]{1,0:T(8,128)S(1)} %fusion.80) | copy-start | bytes 98308
  416.9 161.5 %all-reduce.12.cloned.1.call-start = ((), (), s32[]{:S(2)}) async-start(), calls=%async_computation.6 | async-start | bytes 524288 | tf_op jit(solution)/shard_map/psum | solution.py:29
  484.6 6.7 collective-permute-start.7
  491.3 6.6 collective-permute-start.8
  497.9 6.8 %collective-permute-start.9 = (f32[32,256]{1,0:T(8,128)S(1)}, f32[32,256]{1,0:T(8,128)S(1)}, u32[]{:S(2)}, u32[]{:S(2)}) collective-permute-start(f32[32,256]{1,0:T(8,128)S(1)} %collective-permute-done.8), channel_id=1, source_target_pairs={{0,4},{4,8},{8,12},{12,16},{16,20},{20,24},{24,28},{28,0},{1,5},{5... | collective-permute-start | bytes 98312 | tf_op jit(solution)/shard_map/ppermute | solution.py:57
  504.7 6.6 collective-permute-start.10
  511.4 6.6 collective-permute-start.11
  518.0 6.6 collective-permute-start.12
  524.6 6.6 collective-permute-start.13
  537.2 42.4 %copy-start.2 = (f32[256,256]{1,0:T(8,128)}, f32[256,256]{1,0:T(8,128)S(1)}, u32[]{:S(2)}) copy-start(f32[256,256]{1,0:T(8,128)S(1)} %broadcast_divide_fusion) | copy-start | bytes 786436
  548.5 91.6 %reduce-scatter.14.cloned.1.call-start = ((), (), s32[]{:S(2)}) async-start(), calls=%async_computation.9 | async-start | bytes 163840
  669.7 0.7 copy-start.4
Sparse Core Ops, SparseCore 0:
  10.9 34.9 all-reduce.7
  49.3 71.0 all-reduce.5
  188.1 61.6 reduce-scatter.9
  306.6 29.9 all-reduce.9
  417.0 64.7 reduce-scatter.11
  548.6 29.8 all-reduce.11
  581.4 19.8 reduce-scatter.13
